TPU v7x, 32 devices: a whole 2x2x4 slice. The times are simulated.
32 devices in a mesh: cell: 8 (over z, x), grp: 4 (over y, core).
Axes of the slice: x: 2, y: 2, z: 4, core: 2. Of those that a mesh axis runs over, the one named last changes fastest.
Arguments:
- atom_sites: float32 [3, 16384], P(None, ('cell', 'grp')), may hold values from 0 to 8, as said below
- grid_points: float32 [3, 12288], P(None, ('cell', 'grp')), may hold values from 0 to 8, as said below
- dipole_guess: float32 [3, 16384], P(None, ('cell', 'grp')), may hold values from -2 to 2
- fixed_field: float32 [3, 16384], P(None, ('cell', 'grp')), may hold values from -1800 to 1800
- polarisability: float32 [16384], P(('cell', 'grp')), may hold values from 0.0005 to 0.002
- base_charge: float32 [12288], P(('cell', 'grp')), may hold values from -12 to 12
- response: float32 [12288], P(('cell', 'grp')), may hold values from 0.02 to 0.2
- near_blocks: int32 [128, 8], P(('cell', 'grp')), may hold values from 0 to 47, as said below
- grid_blocks: int32 [128, 4], P(('cell', 'grp')), may hold values from 0 to 35, as said below
- source_blocks: int32 [96, 8], P(('cell', 'grp')), may hold values from 0 to 47, as said below
Outputs:
- dipoles: float32 [3, 16384], P(None, ('cell', 'grp'))
- qm_charges: float32 [12288], P(('cell', 'grp'))
Inputs may be any that keep to these rules, and one draw needn't show every extreme that they name: `atom_sites`: atom a has first coordinate in [c, c + 1) with c = a // 2048, the other two in [0, 1). `grid_points`: grid point g has first coordinate in [c, c + 1) with c = g // 1536, the other two in [0, 1). `near_blocks`: each row holds 8 distinct MM window indices, never the block's own index 16 + b % 16. `grid_blocks`: each row holds 4 distinct grid window indices. `source_blocks`: each row holds 8 distinct MM window indices.
All inputs are finite; a program needn't handle non-finite values.
Results may differ from a plain program's by a relative error of at most 0.0003.
Values sent between devices are 32-bit elements; how exact they have to be, the bound alone decides.
A program may use at most 64 MiB of HBM per device.

v0:
```python
import functools
import math

import jax
import jax.numpy as jnp
from jax import lax
from jax.experimental import pallas as pl
from jax.experimental.pallas import tpu as pltpu
from jax.sharding import PartitionSpec as P

BLOCK = 128
SUB = 8
GROUPS = BLOCK // SUB
UNROLL = 8
HALVES = GROUPS // UNROLL
ITERS = 3
MESH = pl.DeviceIdType.MESH

soften_sq = 0.04


def round_up(n, m):
    return (n + m - 1) // m * m


def body(dims, *refs):
    cells, grps, na, ng, nb, nq, nm = dims
    args, (out_dip, out_q), held = refs[:10], refs[10:12], refs[12:22]
    near_s, grid_s, source_s, sites, points, guess, fixed, pol, base, resp = held
    stat = refs[22]
    dyn = refs[23 : 23 + ITERS]
    tab = refs[23 + ITERS : 23 + 2 * ITERS]
    rest = refs[23 + 2 * ITERS :]
    tgt_a, tgt_g, geo, cgeo, pgeo, fld, selfs = rest[:7]
    load_sem, stat_send, stat_recv, dyn_send, dyn_recv, far_send, far_recv = rest[7:]
    cell = lax.axis_index("cell")
    grp = lax.axis_index("grp")
    has_prev = cell > 0
    has_next = cell < cells - 1
    nk = nb + 1
    own = grps + grp
    cell_f = cell.astype(jnp.float32)
    centre = (cell_f + 0.5, 0.5, 0.5)

    def vec_row(ref, a, b):
        return ref[a : a + 1, b * BLOCK : (b + 1) * BLOCK]

    def flat_row(ref, b):
        return ref[b * BLOCK : (b + 1) * BLOCK].reshape(1, BLOCK)

    lanes = lax.broadcasted_iota(jnp.int32, (SUB, BLOCK), 1)
    subs = lax.broadcasted_iota(jnp.int32, (SUB, BLOCK), 0)
    diag = lanes - subs

    for it in range(ITERS):
        tab[it][...] = jnp.zeros_like(tab[it])

    @pl.when(jnp.logical_not(has_prev))
    def _():
        for p in range(grps):
            stat[p] = jnp.zeros(stat.shape[1:], jnp.float32)
            for it in range(ITERS):
                dyn[it][p] = jnp.zeros(dyn[it].shape[1:], jnp.float32)

    @pl.when(jnp.logical_not(has_next))
    def _():
        for p in range(2 * grps, 3 * grps):
            stat[p] = jnp.zeros(stat.shape[1:], jnp.float32)
            for it in range(ITERS):
                dyn[it][p] = jnp.zeros(dyn[it].shape[1:], jnp.float32)

    barrier = pltpu.get_barrier_semaphore()

    def greet(c, g):
        pl.semaphore_signal(barrier, inc=1, device_id=(c, g), device_id_type=MESH)

    def each_other_cell(act):
        def step(n, carry):
            c = lax.rem(cell + n, cells)
            for d in range(grps):
                act(c, lax.rem(grp + d, grps))
            return carry

        lax.fori_loop(1, cells, step, 0)

    each_other_cell(greet)
    for d in range(1, grps):
        greet(cell, lax.rem(grp + d, grps))

    loads = [
        pltpu.make_async_copy(src, dst, load_sem.at[n])
        for n, (src, dst) in enumerate(zip(args, held))
    ]
    for load in loads:
        load.start()
    for load in loads:
        load.wait()

    for a in range(3):
        for b in range(na):
            stat[own, a * na + b : a * na + b + 1, :] = vec_row(sites, a, b)
            dyn[0][own, a * na + b : a * na + b + 1, :] = vec_row(guess, a, b)
        for b in range(ng):
            r = 3 * na + a * ng + b
            stat[own, r : r + 1, :] = vec_row(points, a, b)
    for b in range(ng):
        dyn[0][own, 3 * na + b : 3 * na + b + 1, :] = flat_row(base, b)

    for a in range(3):
        for b in range(na):
            tgt_a[b, a] = jnp.transpose(jnp.broadcast_to(vec_row(sites, a, b), (BLOCK, BLOCK)))
        for b in range(ng):
            tgt_g[b, a] = jnp.transpose(jnp.broadcast_to(vec_row(points, a, b), (BLOCK, BLOCK)))

    def inverse_of(dx, dy, dz):
        return lax.rsqrt(dx * dx + dy * dy + dz * dz + soften_sq)

    def store_dipole_pair(slot, targets, source, self_mask):
        dx, dy, dz = (t - s for t, s in zip(targets, source))
        inv = inverse_of(dx, dy, dz)
        cube = inv * inv * inv
        weight = cube * lax.rsqrt(inv) * math.sqrt(3.0)
        geo[slot] = dx * weight
        geo[slot + 1] = dy * weight
        geo[slot + 2] = dz * weight
        geo[slot + 3] = cube if self_mask is None else jnp.where(self_mask, 0.0, cube)

    def store_charge_pair(ref, slot, targets, source):
        dx, dy, dz = (t - s for t, s in zip(targets, source))
        inv = inverse_of(dx, dy, dz)
        cube = inv * inv * inv
        ref[slot] = dx * cube
        ref[slot + 1] = dy * cube
        ref[slot + 2] = dz * cube

    def column_sum(x):
        return jnp.sum(x, axis=0, keepdims=True)

    def wide(row):
        return jnp.broadcast_to(row, (SUB, BLOCK))

    def targets_of(ref, b, group):
        return [ref[b, a, pl.ds(group * SUB, SUB), :] for a in range(3)]

    for b in range(na):
        source = [wide(vec_row(sites, a, b)) for a in range(3)]
        for t in range(GROUPS):
            slot = (b * GROUPS + t) * nk * 4
            store_dipole_pair(slot, targets_of(tgt_a, b, t), source, diag == t * SUB)

    pl.semaphore_wait(barrier, cells * grps - 1)

    def piece_copy(buf, send, recv, slot, c, g):
        return pltpu.make_async_remote_copy(
            src_ref=buf.at[own],
            dst_ref=buf.at[slot * grps + grp],
            send_sem=send.at[slot * grps + g],
            recv_sem=recv.at[slot * grps + grp],
            device_id=(c, g),
            device_id_type=MESH,
        )

    def for_peers(buf, send, recv, act):
        for d in range(1, grps):
            g = lax.rem(grp + d, grps)
            act(piece_copy(buf, send, recv, 1, cell, g))

    def for_neighbours(buf, send, recv, act):
        @pl.when(has_prev)
        def _():
            for d in range(grps):
                g = lax.rem(grp + d, grps)
                act(piece_copy(buf, send, recv, 2, cell - 1, g))

        @pl.when(has_next)
        def _():
            for d in range(grps):
                g = lax.rem(grp + d, grps)
                act(piece_copy(buf, send, recv, 0, cell + 1, g))

    def arrival(buf, send, recv, p, c, g):
        pltpu.make_async_remote_copy(
            src_ref=buf.at[p],
            dst_ref=buf.at[p],
            send_sem=send.at[p],
            recv_sem=recv.at[p],
            device_id=(c, g),
            device_id_type=MESH,
        ).wait_recv()

    def peers_arrive(buf, send, recv):
        for d in range(1, grps):
            g = lax.rem(grp + d, grps)
            arrival(buf, send, recv, grps + g, cell, g)

    def neighbours_arrive(buf, send, recv):
        @pl.when(has_prev)
        def _():
            for g in range(grps):
                arrival(buf, send, recv, g, cell - 1, g)

        @pl.when(has_next)
        def _():
            for g in range(grps):
                arrival(buf, send, recv, 2 * grps + g, cell + 1, g)

    def start(copy):
        copy.start()

    def far_row(it, c, g):
        return tab[it].at[pl.ds(g * cells + c, 1)]

    def far_copy(it, c, g):
        return pltpu.make_async_remote_copy(
            src_ref=far_row(it, cell, grp),
            dst_ref=far_row(it, cell, grp),
            send_sem=far_send.at[it],
            recv_sem=far_recv.at[it],
            device_id=(c, g),
            device_id_type=MESH,
        )

    def far_all(it):
        rows = tab[it].at[pl.ds(0, (cells - 1) * grps)]
        return pltpu.make_async_remote_copy(
            src_ref=rows,
            dst_ref=rows,
            send_sem=far_send.at[it],
            recv_sem=far_recv.at[it],
            device_id=(lax.rem(cell + 1, cells), grp),
            device_id_type=MESH,
        )

    def own_sums(it):
        mine = dyn[it][own]
        rows = [column_sum(mine[a * na : (a + 1) * na]) for a in range(3)]
        q = mine[3 * na : 3 * na + ng]
        rows.append(column_sum(q))
        for a in range(3):
            r = 3 * na + a * ng
            rows.append(column_sum(q * (stat[own, r : r + ng, :] - centre[a])))
        tile = jnp.zeros((SUB, BLOCK), jnp.float32)
        for n, row in enumerate(rows):
            tile = jnp.where(subs == n, wide(row), tile)
        sums = jnp.sum(tile, axis=1, keepdims=True)
        tab[it][grp * cells + cell] = column_sum(jnp.where(diag == 0, sums, 0.0))

    def far_sums(it):
        total = tab[it][0:cells, 0, :]
        for g in range(1, grps):
            total = total + tab[it][g * cells : (g + 1) * cells, 0, :]
        return [jnp.broadcast_to(total[:, n : n + 1], (cells, BLOCK)) for n in range(7)]

    def mm_place(w):
        return lax.div(w, na), lax.rem(w, na)

    def grid_place(w):
        return lax.div(w, ng), lax.rem(w, ng)

    def site_rows(w):
        p, lb = mm_place(w)
        return [wide(stat[p, pl.ds(a * na + lb, 1), :]) for a in range(3)]

    def point_rows(w):
        p, lb = grid_place(w)
        return [wide(stat[p, pl.ds(3 * na + a * ng + lb, 1), :]) for a in range(3)]

    def geometry_atoms(i, carry):
        b = lax.div(i, HALVES)
        first = lax.rem(i, HALVES) * UNROLL
        for k in range(nb):
            source = site_rows(near_s[b, k])
            for t in range(UNROLL):
                slot = ((i * UNROLL + t) * nk + k + 1) * 4
                store_dipole_pair(slot, targets_of(tgt_a, b, first + t), source, None)
        for k in range(nq):
            source = point_rows(grid_s[b, k])
            for t in range(UNROLL):
                slot = ((i * UNROLL + t) * nq + k) * 3
                store_charge_pair(cgeo, slot, targets_of(tgt_a, b, first + t), source)
        return carry

    def geometry_grid(i, carry):
        b = lax.div(i, HALVES)
        first = lax.rem(i, HALVES) * UNROLL
        for k in range(nm):
            source = site_rows(source_s[b, k])
            for t in range(UNROLL):
                slot = ((i * UNROLL + t) * nm + k) * 3
                store_charge_pair(pgeo, slot, targets_of(tgt_g, b, first + t), source)
        return carry

    def self_atoms(it, i, carry):
        b = lax.div(i, HALVES)
        mu = [wide(dyn[it][own, pl.ds(a * na + b, 1), :]) for a in range(3)]
        for t in range(UNROLL):
            slot = (i * UNROLL + t) * nk * 4
            u = [geo[slot + a] for a in range(3)]
            cube = geo[slot + 3]
            proj = u[0] * mu[0] + u[1] * mu[1] + u[2] * mu[2]
            for a in range(3):
                selfs[(i * UNROLL + t) * 3 + a] = u[a] * proj - cube * mu[a]
        return carry

    def near_atoms(it, i, carry):
        b = lax.div(i, HALVES)
        first = lax.rem(i, HALVES) * UNROLL
        acc = [[selfs[(i * UNROLL + t) * 3 + a] for a in range(3)] for t in range(UNROLL)]
        for k in range(1, nk):
            p, lb = mm_place(near_s[b, k - 1])
            mu = [wide(dyn[it][p, pl.ds(a * na + lb, 1), :]) for a in range(3)]
            for t in range(UNROLL):
                slot = ((i * UNROLL + t) * nk + k) * 4
                u = [geo[slot + a] for a in range(3)]
                cube = geo[slot + 3]
                proj = u[0] * mu[0] + u[1] * mu[1] + u[2] * mu[2]
                for a in range(3):
                    term = u[a] * proj - cube * mu[a]
                    acc[t][a] = acc[t][a] + term
        for k in range(nq):
            p, lb = grid_place(grid_s[b, k])
            q = wide(dyn[it][p, pl.ds(3 * na + lb, 1), :])
            for t in range(UNROLL):
                slot = ((i * UNROLL + t) * nq + k) * 3
                for a in range(3):
                    acc[t][a] = acc[t][a] + cgeo[slot + a] * q
        out = []
        for a in range(3):
            row = jnp.zeros((SUB, BLOCK), jnp.float32)
            for t in range(UNROLL):
                total = jnp.sum(acc[t][a], axis=1, keepdims=True)
                row = jnp.where(diag == (first + t) * SUB, total, row)
            out.append(row)
        for a in range(3):
            fld[i * 3 + a] = out[a]
        return carry

    def near_grid(it, i, carry):
        b = lax.div(i, HALVES)
        first = lax.rem(i, HALVES) * UNROLL
        acc = [None] * UNROLL
        for k in range(nm):
            p, lb = mm_place(source_s[b, k])
            mu = [wide(dyn[it][p, pl.ds(a * na + lb, 1), :]) for a in range(3)]
            for t in range(UNROLL):
                slot = ((i * UNROLL + t) * nm + k) * 3
                term = pgeo[slot] * mu[0] + pgeo[slot + 1] * mu[1] + pgeo[slot + 2] * mu[2]
                acc[t] = term if k == 0 else acc[t] + term
        row = jnp.zeros((SUB, BLOCK), jnp.float32)
        for t in range(UNROLL):
            total = jnp.sum(acc[t], axis=1, keepdims=True)
            row = jnp.where(diag == (first + t) * SUB, total, row)
        fld[na * HALVES * 3 + i] = row
        return carry

    def far_geometry(row_of):
        c = lax.broadcasted_iota(jnp.int32, (cells, BLOCK), 0)
        dx = row_of(0) - (c.astype(jnp.float32) + 0.5)
        dy = jnp.broadcast_to(row_of(1) - 0.5, (cells, BLOCK))
        dz = jnp.broadcast_to(row_of(2) - 0.5, (cells, BLOCK))
        inv = inverse_of(dx, dy, dz)
        cube = jnp.where(jnp.abs(c - cell) >= 2, inv * inv * inv, 0.0)
        return (dx, dy, dz), cube, cube * inv * inv * 3.0

    for_neighbours(stat, stat_send, stat_recv, start)
    for_peers(stat, stat_send, stat_recv, start)
    for_neighbours(dyn[0], dyn_send.at[0], dyn_recv.at[0], start)
    for_peers(dyn[0], dyn_send.at[0], dyn_recv.at[0], start)

    for it in range(ITERS):
        send, recv = dyn_send.at[it], dyn_recv.at[it]
        if it > 0:
            for_neighbours(dyn[it], send, recv, start)
            for_peers(dyn[it], send, recv, start)
        own_sums(it)
        each_other_cell(lambda c, g: far_copy(it, c, g).start())
        lax.fori_loop(0, na * HALVES, functools.partial(self_atoms, it), 0)
        if it == 0:
            peers_arrive(stat, stat_send, stat_recv)
            neighbours_arrive(stat, stat_send, stat_recv)
            lax.fori_loop(0, na * HALVES, geometry_atoms, 0)
            lax.fori_loop(0, ng * HALVES, geometry_grid, 0)
        peers_arrive(dyn[it], send, recv)
        neighbours_arrive(dyn[it], send, recv)
        lax.fori_loop(0, na * HALVES, functools.partial(near_atoms, it), 0)
        lax.fori_loop(0, ng * HALVES, functools.partial(near_grid, it), 0)
        far_all(it).wait_recv()
        sums = far_sums(it)
        moments = [sums[a] + sums[4 + a] for a in range(3)]
        for b in range(na):
            delta, cube, fifth = far_geometry(lambda a: vec_row(sites, a, b))
            radial = fifth * (moments[0] * delta[0] + moments[1] * delta[1] + moments[2] * delta[2])
            radial = radial + sums[3] * cube
            for a in range(3):
                far = column_sum(radial * delta[a] - moments[a] * cube)
                near = fld[b * HALVES * 3 + a]
                for h in range(1, HALVES):
                    near = near + fld[(b * HALVES + h) * 3 + a]
                new = flat_row(pol, b) * (vec_row(fixed, a, b) + (column_sum(near) + far))
                if it + 1 < ITERS:
                    dyn[it + 1][own, a * na + b : a * na + b + 1, :] = new
                else:
                    out_dip[a : a + 1, b * BLOCK : (b + 1) * BLOCK] = new
        for b in range(ng):
            delta, cube, _ = far_geometry(lambda a: vec_row(points, a, b))
            proj = sums[0] * delta[0] + sums[1] * delta[1] + sums[2] * delta[2]
            far = column_sum(proj * cube)
            slot = na * HALVES * 3 + b * HALVES
            near = fld[slot]
            for h in range(1, HALVES):
                near = near + fld[slot + h]
            new = flat_row(base, b) - flat_row(resp, b) * (column_sum(near) + far)
            if it + 1 < ITERS:
                dyn[it + 1][own, 3 * na + b : 3 * na + b + 1, :] = new
            else:
                out_q[b * BLOCK : (b + 1) * BLOCK] = new.reshape(BLOCK)

    def finish(copy):
        copy.wait_send()

    for_peers(stat, stat_send, stat_recv, finish)
    for_neighbours(stat, stat_send, stat_recv, finish)
    for it in range(ITERS):
        for_peers(dyn[it], dyn_send.at[it], dyn_recv.at[it], finish)
        for_neighbours(dyn[it], dyn_send.at[it], dyn_recv.at[it], finish)
        far_all(it).wait_send()


def solution(mesh):
    cells, grps = mesh.shape["cell"], mesh.shape["grp"]

    def step(sites, points, guess, fixed, pol, base, resp, near, grid, source):
        na, nb = near.shape
        nq = grid.shape[1]
        ng, nm = source.shape
        stat_rows = round_up(3 * na + 3 * ng, SUB)
        dyn_rows = round_up(3 * na + ng, SUB)
        f32 = jnp.float32
        args = (near, grid, source, sites, points, guess, fixed, pol, base, resp)
        vmem = pl.BlockSpec(memory_space=pltpu.VMEM)
        dma = pltpu.SemaphoreType.DMA
        return pl.pallas_call(
            functools.partial(body, (cells, grps, na, ng, nb, nq, nm)),
            out_shape=(
                jax.ShapeDtypeStruct(sites.shape, f32),
                jax.ShapeDtypeStruct(base.shape, f32),
            ),
            in_specs=[pl.BlockSpec(memory_space=pl.ANY)] * 10,
            out_specs=(vmem, vmem),
            scratch_shapes=[pltpu.SMEM(x.shape, x.dtype) for x in args[:3]]
            + [pltpu.VMEM(x.shape, x.dtype) for x in args[3:]]
            + [pltpu.VMEM((3 * grps, stat_rows, BLOCK), f32)]
            + [pltpu.VMEM((3 * grps, dyn_rows, BLOCK), f32) for _ in range(ITERS)]
            + [pltpu.VMEM((cells * grps, 1, BLOCK), f32) for _ in range(ITERS)]
            + [
                pltpu.VMEM((na, 3, BLOCK, BLOCK), f32),
                pltpu.VMEM((ng, 3, BLOCK, BLOCK), f32),
                pltpu.VMEM((na * GROUPS * (nb + 1) * 4, SUB, BLOCK), f32),
                pltpu.VMEM((na * GROUPS * nq * 3, SUB, BLOCK), f32),
                pltpu.VMEM((ng * GROUPS * nm * 3, SUB, BLOCK), f32),
                pltpu.VMEM(((na * 3 + ng) * HALVES, SUB, BLOCK), f32),
                pltpu.VMEM((na * GROUPS * 3, SUB, BLOCK), f32),
                dma((10,)),
                dma((3 * grps,)),
                dma((3 * grps,)),
                dma((ITERS, 3 * grps)),
                dma((ITERS, 3 * grps)),
                dma((ITERS,)),
                dma((ITERS,)),
            ],
            compiler_params=pltpu.CompilerParams(collective_id=0, has_side_effects=True),
        )(*args)

    pair = P(("cell", "grp"))
    wide = P(None, ("cell", "grp"))
    tall = P(("cell", "grp"), None)
    return jax.shard_map(
        step,
        mesh=mesh,
        in_specs=(wide, wide, wide, wide, pair, pair, pair, tall, tall, tall),
        out_specs=(wide, pair),
        check_vma=False,
    )
```

profile of v0, /device:TPU:0, one launch (start us, length us, event | category | flops | bytes accessed | tf_op | source)
XLA Modules:
  0.0 35.3 jit_solution(2625388677620601132)
XLA Ops:
  0.6 32.7 %shard_map.113 = (f32[3,512]{1,0:T(4,128)}, f32[384]{0:T(512)}) custom-call(s32[4,8]{1,0:T(4,128)} %refs_0_.1, s32[4,4]{1,0:T(4,128)} %refs_1_.1, s32[3,8]{1,0:T(4,128)} %refs_2_.1, f32[3,512]{1,0:T(4,128)} %refs_3_.1, f32[3,384]{1,0:T(4,128)} %refs_4_.1, f32[3,512]{1,0:T(4,128)} %refs_5_.1, f32[3,512]{1,0:T(4,128)} %refs_6_.1, f32[512]{0:T(512)} %refs_7_.1, ...), custom_call_target="tpu_custom_call" | custom-call | tf_op jit(solution)/shard_map/pallas_call | solution.py:442
  33.4 0.0 copy-start
  33.4 1.3 %copy.14 = f32[3,512]{1,0:T(4,128)} copy(f32[3,512]{1,0:T(4,128)} %get-tuple-element.4) | data formatting | bytes 12288
  34.7 0.0 copy-done
  34.7 0.6 %copy.15 = f32[384]{0:T(512)} copy(f32[384]{0:T(512)S(1)} %copy-done) | data formatting | bytes 3072
Async XLA Ops:
  33.4 1.3 %copy-start = (f32[384]{0:T(512)S(1)}, f32[384]{0:T(512)}, u32[]{:S(2)}) copy-start(f32[384]{0:T(512)} %get-tuple-element.5) | copy-start | bytes 4612
where the time goes:
time: 35.4 us; the launch traced here: 35.3 us
  Pallas kernels  32.7 us (92%)
  local copies, waits for them, and re-layouts  1.88 us (5%)
  between operations  0.65 us (2%)
    pallas_call x1, Pallas kernels, step(): pl.pallas_call(functools.partial(body, (cells, grps, na, ng, nb, nq, nm))...  32.7 us
    unnamed x4, local copies, waits for them, and re-layouts  1.88 us

commit v1 on v0

v1 whole, which is shorter than its diff:
```python
import functools
import math

import jax
import jax.numpy as jnp
from jax import lax
from jax.experimental import pallas as pl
from jax.experimental.pallas import tpu as pltpu
from jax.sharding import PartitionSpec as P

BLOCK = 128
SUB = 8
GROUPS = BLOCK // SUB
UNROLL = 8
HALVES = GROUPS // UNROLL
ITERS = 3
MESH = pl.DeviceIdType.MESH

soften_sq = 0.04


def body(dims, *refs):
    cells, grps, na, ng, nb, nq, nm = dims
    args, (out_dip, out_q), held = refs[:10], refs[10:12], refs[12:22]
    near_s, grid_s, source_s, sites, points, guess, fixed, pol, base, resp = held
    sit, pts = refs[22:24]
    mus = refs[24 : 24 + ITERS]
    chg = (None,) + refs[24 + ITERS : 23 + 2 * ITERS]
    tab = refs[23 + 2 * ITERS : 23 + 3 * ITERS]
    rest = refs[23 + 3 * ITERS :]
    tgt_a, tgt_g, geo, sgeo, cgeo, pgeo, fgeo_a, fgeo_g, acc_a, acc_g = rest[:10]
    load_sem, send_sem, recv_sem, far_send, far_recv = rest[10:]
    cell = lax.axis_index("cell")
    grp = lax.axis_index("grp")
    has_prev = cell > 0
    has_next = cell < cells - 1
    own = grps + grp
    cell_f = cell.astype(jnp.float32)
    centre = (cell_f + 0.5, 0.5, 0.5)
    pieces = 3 * grps
    order = sorted(range(grps), key=lambda d: (abs(2 * d - grps), d))

    site_msg = (sit, 3 * na, 0)
    point_msg = (pts, 4 * ng, 1)
    mu_msg = [(mus[it], 3 * na, 2 + it) for it in range(ITERS)]
    charge_msg = [None] + [(chg[it], ng, 1 + ITERS + it) for it in range(1, ITERS)]

    def vec_row(ref, a, b):
        return ref[a : a + 1, b * BLOCK : (b + 1) * BLOCK]

    def flat_row(ref, b):
        return ref[b * BLOCK : (b + 1) * BLOCK].reshape(1, BLOCK)

    lanes = lax.broadcasted_iota(jnp.int32, (SUB, BLOCK), 1)
    subs = lax.broadcasted_iota(jnp.int32, (SUB, BLOCK), 0)
    diag = lanes - subs

    barrier = pltpu.get_barrier_semaphore()

    def greet(c, g):
        pl.semaphore_signal(barrier, inc=1, device_id=(c, g), device_id_type=MESH)

    def each_other_cell(act):
        def step(n, carry):
            c = lax.rem(cell + n, cells)
            for d in range(grps):
                act(c, lax.rem(grp + d, grps))
            return carry

        lax.fori_loop(1, cells, step, 0)

    loads = [
        pltpu.make_async_copy(src, dst, load_sem.at[n])
        for n, (src, dst) in enumerate(zip(args, held))
    ]
    for n in (3, 5, 4, 8, 0, 1, 2, 6, 7, 9):
        loads[n].start()
    each_other_cell(greet)
    for d in range(1, grps):
        greet(cell, lax.rem(grp + d, grps))

    def clear(slot):
        for buf, rows, _ in [site_msg, point_msg] + mu_msg + charge_msg[1:]:
            buf[slot * grps * rows : (slot + 1) * grps * rows] = jnp.zeros((grps * rows, 1, BLOCK), jnp.float32)

    for it in range(ITERS):
        for g in range(grps):
            tab[it][g * cells + cell] = jnp.zeros((1, BLOCK), jnp.float32)
    pl.when(jnp.logical_not(has_prev))(lambda: clear(0))
    pl.when(jnp.logical_not(has_next))(lambda: clear(2))

    for n in (3, 5, 4, 8):
        loads[n].wait()

    for b in range(na):
        for a in range(3):
            sit[own * 3 * na + b * 3 + a] = vec_row(sites, a, b)
            mus[0][own * 3 * na + b * 3 + a] = vec_row(guess, a, b)
    for b in range(ng):
        for a in range(3):
            pts[own * 4 * ng + b * 4 + a] = vec_row(points, a, b)
        pts[own * 4 * ng + b * 4 + 3] = flat_row(base, b)

    def inverse_of(dx, dy, dz):
        return lax.rsqrt(dx * dx + dy * dy + dz * dz + soften_sq)

    def store_dipole_pair(ref, slot, targets, source, self_mask):
        dx, dy, dz = (t - s for t, s in zip(targets, source))
        inv = inverse_of(dx, dy, dz)
        cube = inv * inv * inv
        weight = cube * lax.rsqrt(inv) * math.sqrt(3.0)
        ref[slot] = dx * weight
        ref[slot + 1] = dy * weight
        ref[slot + 2] = dz * weight
        ref[slot + 3] = cube if self_mask is None else jnp.where(self_mask, 0.0, cube)

    def store_charge_pair(ref, slot, targets, source):
        dx, dy, dz = (t - s for t, s in zip(targets, source))
        inv = inverse_of(dx, dy, dz)
        cube = inv * inv * inv
        ref[slot] = dx * cube
        ref[slot + 1] = dy * cube
        ref[slot + 2] = dz * cube

    def column_sum(x):
        return jnp.sum(x, axis=0, keepdims=True)

    def wide(row):
        return jnp.broadcast_to(row, (SUB, BLOCK))

    def targets_of(ref, b, group):
        return [ref[b, a, pl.ds(group * SUB, SUB), :] for a in range(3)]

    def piece_copy(msg, slot, c, g):
        buf, rows, kind = msg
        return pltpu.make_async_remote_copy(
            src_ref=buf.at[pl.ds(own * rows, rows)],
            dst_ref=buf.at[pl.ds((slot * grps + grp) * rows, rows)],
            send_sem=send_sem.at[kind, slot * grps + g],
            recv_sem=recv_sem.at[kind, slot * grps + grp],
            device_id=(c, g),
            device_id_type=MESH,
        )

    def for_all(msg, act):
        @pl.when(has_prev)
        def _():
            for d in order:
                g = lax.rem(grp + d, grps)
                act(piece_copy(msg, 2, cell - 1, g))

        @pl.when(has_next)
        def _():
            for d in order:
                g = lax.rem(grp + d, grps)
                act(piece_copy(msg, 0, cell + 1, g))

        for d in order:
            if d:
                g = lax.rem(grp + d, grps)
                act(piece_copy(msg, 1, cell, g))

    def arrival(msg, p, c, g):
        buf, rows, kind = msg
        pltpu.make_async_remote_copy(
            src_ref=buf.at[pl.ds(p * rows, rows)],
            dst_ref=buf.at[pl.ds(p * rows, rows)],
            send_sem=send_sem.at[kind, p],
            recv_sem=recv_sem.at[kind, p],
            device_id=(c, g),
            device_id_type=MESH,
        ).wait_recv()

    def all_arrive(msg):
        for d in range(1, grps):
            g = lax.rem(grp + d, grps)
            arrival(msg, grps + g, cell, g)

        @pl.when(has_prev)
        def _():
            for g in range(grps):
                arrival(msg, g, cell - 1, g)

        @pl.when(has_next)
        def _():
            for g in range(grps):
                arrival(msg, 2 * grps + g, cell + 1, g)

    def start(copy):
        copy.start()

    def finish(copy):
        copy.wait_send()

    def far_row(it, c, g):
        return tab[it].at[pl.ds(g * cells + c, 1)]

    def far_copy(it, c, g):
        return pltpu.make_async_remote_copy(
            src_ref=far_row(it, cell, grp),
            dst_ref=far_row(it, cell, grp),
            send_sem=far_send.at[it],
            recv_sem=far_recv.at[it],
            device_id=(c, g),
            device_id_type=MESH,
        )

    def far_all(it):
        rows = tab[it].at[pl.ds(0, (cells - 1) * grps)]
        return pltpu.make_async_remote_copy(
            src_ref=rows,
            dst_ref=rows,
            send_sem=far_send.at[it],
            recv_sem=far_recv.at[it],
            device_id=(lax.rem(cell + 1, cells), grp),
            device_id_type=MESH,
        )

    def charge_row(it, w):
        return pts[w * 4 + 3] if it == 0 else chg[it][w]

    def own_sums(it):
        rows = []
        for a in range(3):
            total = mus[it][own * 3 * na + a]
            for b in range(1, na):
                total = total + mus[it][own * 3 * na + b * 3 + a]
            rows.append(total)
        q = [charge_row(it, own * ng + b) for b in range(ng)]
        rows.append(functools.reduce(jnp.add, q))
        for a in range(3):
            rows.append(functools.reduce(jnp.add, [q[b] * (vec_row(points, a, b) - centre[a]) for b in range(ng)]))
        tile = jnp.zeros((SUB, BLOCK), jnp.float32)
        for n, row in enumerate(rows):
            tile = jnp.where(subs == n, wide(row), tile)
        sums = jnp.sum(tile, axis=1, keepdims=True)
        tab[it][grp * cells + cell] = column_sum(jnp.where(diag == 0, sums, 0.0))

    def far_sums(it):
        total = tab[it][0:cells, 0, :]
        for g in range(1, grps):
            total = total + tab[it][g * cells : (g + 1) * cells, 0, :]
        return [jnp.broadcast_to(total[:, n : n + 1], (cells, BLOCK)) for n in range(7)]

    def site_rows(w):
        return [wide(sit[w * 3 + a]) for a in range(3)]

    def point_rows(w):
        return [wide(pts[w * 4 + a]) for a in range(3)]

    def mu_rows(it, w):
        return [wide(mus[it][w * 3 + a]) for a in range(3)]

    def near_geometry(i, carry):
        b = lax.div(i, HALVES)
        first = lax.rem(i, HALVES) * UNROLL
        for k in range(nb):
            source = site_rows(near_s[b, k])
            for t in range(UNROLL):
                slot = ((i * UNROLL + t) * nb + k) * 4
                store_dipole_pair(geo, slot, targets_of(tgt_a, b, first + t), source, None)
        return carry

    def charge_geometry(i, carry):
        b = lax.div(i, HALVES)
        first = lax.rem(i, HALVES) * UNROLL
        for k in range(nq):
            source = point_rows(grid_s[b, k])
            for t in range(UNROLL):
                slot = ((i * UNROLL + t) * nq + k) * 3
                store_charge_pair(cgeo, slot, targets_of(tgt_a, b, first + t), source)
        return carry

    def grid_geometry(i, carry):
        b = lax.div(i, HALVES)
        first = lax.rem(i, HALVES) * UNROLL
        for k in range(nm):
            source = site_rows(source_s[b, k])
            for t in range(UNROLL):
                slot = ((i * UNROLL + t) * nm + k) * 3
                store_charge_pair(pgeo, slot, targets_of(tgt_g, b, first + t), source)
        return carry

    def self_atoms(it, i, carry):
        b = lax.div(i, HALVES)
        mu = mu_rows(it, own * na + b)
        for t in range(UNROLL):
            slot = (i * UNROLL + t) * 4
            u = [sgeo[slot + a] for a in range(3)]
            cube = sgeo[slot + 3]
            proj = u[0] * mu[0] + u[1] * mu[1] + u[2] * mu[2]
            for a in range(3):
                acc_a[(i * UNROLL + t) * 3 + a] = u[a] * proj - cube * mu[a]
        return carry

    def near_atoms(it, i, carry):
        b = lax.div(i, HALVES)
        acc = [[acc_a[(i * UNROLL + t) * 3 + a] for a in range(3)] for t in range(UNROLL)]
        for k in range(nb):
            mu = mu_rows(it, near_s[b, k])
            for t in range(UNROLL):
                slot = ((i * UNROLL + t) * nb + k) * 4
                u = [geo[slot + a] for a in range(3)]
                cube = geo[slot + 3]
                proj = u[0] * mu[0] + u[1] * mu[1] + u[2] * mu[2]
                for a in range(3):
                    acc[t][a] = acc[t][a] + (u[a] * proj - cube * mu[a])
        for t in range(UNROLL):
            for a in range(3):
                acc_a[(i * UNROLL + t) * 3 + a] = acc[t][a]
        return carry

    def near_grid(it, i, carry):
        b = lax.div(i, HALVES)
        acc = [None] * UNROLL
        for k in range(nm):
            mu = mu_rows(it, source_s[b, k])
            for t in range(UNROLL):
                slot = ((i * UNROLL + t) * nm + k) * 3
                term = pgeo[slot] * mu[0] + pgeo[slot + 1] * mu[1] + pgeo[slot + 2] * mu[2]
                acc[t] = term if k == 0 else acc[t] + term
        for t in range(UNROLL):
            acc_g[i * UNROLL + t] = acc[t]
        return carry

    def gather_lanes(tiles):
        row = jnp.zeros((SUB, BLOCK), jnp.float32)
        for t, tile in enumerate(tiles):
            total = jnp.sum(tile, axis=1, keepdims=True)
            row = jnp.where(diag == t * SUB, total, row)
        return column_sum(row)

    def atom_fields(it):
        rows = []
        for b in range(na):
            q = [wide(charge_row(it, grid_s[b, k])) for k in range(nq)]
            tiles = [[], [], []]
            for t in range(GROUPS):
                n = b * GROUPS + t
                for a in range(3):
                    terms = [cgeo[(n * nq + k) * 3 + a] * q[k] for k in range(nq)]
                    tiles[a].append(acc_a[n * 3 + a] + functools.reduce(jnp.add, terms))
            rows.append([gather_lanes(tiles[a]) for a in range(3)])
        return rows

    def grid_fields():
        return [gather_lanes([acc_g[b * GROUPS + t] for t in range(GROUPS)]) for b in range(ng)]

    def store_far(ref, n, row_of):
        c = lax.broadcasted_iota(jnp.int32, (cells, BLOCK), 0)
        dx = row_of(0) - (c.astype(jnp.float32) + 0.5)
        dy = jnp.broadcast_to(row_of(1) - 0.5, (cells, BLOCK))
        dz = jnp.broadcast_to(row_of(2) - 0.5, (cells, BLOCK))
        inv = inverse_of(dx, dy, dz)
        cube = jnp.where(jnp.abs(c - cell) >= 2, inv * inv * inv, 0.0)
        for m, x in enumerate((dx, dy, dz, cube, cube * inv * inv * 3.0)):
            ref[n * 5 + m] = x

    def finish_atoms(it, near, sums):
        moments = [sums[a] + sums[4 + a] for a in range(3)]
        for b in range(na):
            delta = [fgeo_a[b * 5 + a] for a in range(3)]
            cube, fifth = fgeo_a[b * 5 + 3], fgeo_a[b * 5 + 4]
            radial = fifth * (moments[0] * delta[0] + moments[1] * delta[1] + moments[2] * delta[2])
            radial = radial + sums[3] * cube
            for a in range(3):
                far = column_sum(radial * delta[a] - moments[a] * cube)
                new = flat_row(pol, b) * (vec_row(fixed, a, b) + (near[b][a] + far))
                if it + 1 < ITERS:
                    mus[it + 1][own * 3 * na + b * 3 + a] = new
                else:
                    out_dip[a : a + 1, b * BLOCK : (b + 1) * BLOCK] = new

    def finish_grid(it, near, sums):
        for b in range(ng):
            delta = [fgeo_g[b * 5 + a] for a in range(3)]
            proj = sums[0] * delta[0] + sums[1] * delta[1] + sums[2] * delta[2]
            far = column_sum(proj * fgeo_g[b * 5 + 3])
            new = flat_row(base, b) - flat_row(resp, b) * (near[b] + far)
            if it + 1 < ITERS:
                chg[it + 1][own * ng + b] = new
            else:
                out_q[b * BLOCK : (b + 1) * BLOCK] = new.reshape(BLOCK)

    atom_steps, grid_steps = na * HALVES, ng * HALVES

    pl.semaphore_wait(barrier, cells * grps - 1)
    for_all(site_msg, start)
    for_all(mu_msg[0], start)
    for_all(point_msg, start)
    own_sums(0)
    each_other_cell(lambda c, g: far_copy(0, c, g).start())

    for a in range(3):
        for b in range(na):
            tgt_a[b, a] = jnp.transpose(jnp.broadcast_to(vec_row(sites, a, b), (BLOCK, BLOCK)))
        for b in range(ng):
            tgt_g[b, a] = jnp.transpose(jnp.broadcast_to(vec_row(points, a, b), (BLOCK, BLOCK)))
    for b in range(na):
        source = [wide(vec_row(sites, a, b)) for a in range(3)]
        for t in range(GROUPS):
            store_dipole_pair(sgeo, (b * GROUPS + t) * 4, targets_of(tgt_a, b, t), source, diag == t * SUB)
    lax.fori_loop(0, atom_steps, functools.partial(self_atoms, 0), 0)
    for b in range(na):
        store_far(fgeo_a, b, lambda a: vec_row(sites, a, b))
    for b in range(ng):
        store_far(fgeo_g, b, lambda a: vec_row(points, a, b))
    for n in (0, 1, 2, 6, 7, 9):
        loads[n].wait()

    all_arrive(site_msg)
    lax.fori_loop(0, atom_steps, near_geometry, 0)

    for it in range(ITERS):
        last = it + 1 == ITERS
        all_arrive(mu_msg[it])
        lax.fori_loop(0, atom_steps, functools.partial(near_atoms, it), 0)
        if last:
            lax.fori_loop(0, grid_steps, functools.partial(near_grid, it), 0)
        if it == 0:
            all_arrive(point_msg)
            lax.fori_loop(0, atom_steps, charge_geometry, 0)
        else:
            all_arrive(charge_msg[it])
        far_all(it).wait_recv()
        sums = far_sums(it)
        finish_atoms(it, atom_fields(it), sums)
        if last:
            finish_grid(it, grid_fields(), sums)
            break
        for_all(mu_msg[it + 1], start)
        if it == 0:
            lax.fori_loop(0, grid_steps, grid_geometry, 0)
        lax.fori_loop(0, grid_steps, functools.partial(near_grid, it), 0)
        finish_grid(it, grid_fields(), sums)
        for_all(charge_msg[it + 1], start)
        own_sums(it + 1)
        each_other_cell(lambda c, g: far_copy(it + 1, c, g).start())
        lax.fori_loop(0, atom_steps, functools.partial(self_atoms, it + 1), 0)

    for msg in [site_msg, point_msg] + mu_msg + charge_msg[1:]:
        for_all(msg, finish)
    for it in range(ITERS):
        far_all(it).wait_send()


def hand_over(dip, q, out_dip, out_q, sem):
    copies = [
        pltpu.make_async_copy(dip, out_dip, sem.at[0]),
        pltpu.make_async_copy(q, out_q, sem.at[1]),
    ]
    for copy in copies:
        copy.start()
    for copy in copies:
        copy.wait()


def solution(mesh):
    cells, grps = mesh.shape["cell"], mesh.shape["grp"]

    def step(sites, points, guess, fixed, pol, base, resp, near, grid, source):
        na, nb = near.shape
        nq = grid.shape[1]
        ng, nm = source.shape
        f32 = jnp.float32
        args = (near, grid, source, sites, points, guess, fixed, pol, base, resp)
        args = tuple(pltpu.with_memory_space_constraint(x, pltpu.HBM) for x in args)
        vmem = pl.BlockSpec(memory_space=pltpu.VMEM)
        hbm = pl.BlockSpec(memory_space=pltpu.HBM)
        dma = pltpu.SemaphoreType.DMA
        outs = (jax.ShapeDtypeStruct(sites.shape, f32), jax.ShapeDtypeStruct(base.shape, f32))

        def rows(n):
            return pltpu.VMEM((3 * grps * n, 1, BLOCK), f32)

        def tiles(n, height=SUB):
            return pltpu.VMEM((n, height, BLOCK), f32)

        kinds = 1 + 2 * ITERS
        results = pl.pallas_call(
            functools.partial(body, (cells, grps, na, ng, nb, nq, nm)),
            out_shape=outs,
            in_specs=[hbm] * 10,
            out_specs=(vmem, vmem),
            scratch_shapes=[pltpu.SMEM(x.shape, x.dtype) for x in args[:3]]
            + [pltpu.VMEM(x.shape, x.dtype) for x in args[3:]]
            + [rows(3 * na), rows(4 * ng)]
            + [rows(3 * na) for _ in range(ITERS)]
            + [rows(ng) for _ in range(ITERS - 1)]
            + [pltpu.VMEM((cells * grps, 1, BLOCK), f32) for _ in range(ITERS)]
            + [
                pltpu.VMEM((na, 3, BLOCK, BLOCK), f32),
                pltpu.VMEM((ng, 3, BLOCK, BLOCK), f32),
                tiles(na * GROUPS * nb * 4),
                tiles(na * GROUPS * 4),
                tiles(na * GROUPS * nq * 3),
                tiles(ng * GROUPS * nm * 3),
                tiles(na * 5, cells),
                tiles(ng * 5, cells),
                tiles(na * GROUPS * 3),
                tiles(ng * GROUPS),
                dma((10,)),
                dma((kinds, 3 * grps)),
                dma((kinds, 3 * grps)),
                dma((ITERS,)),
                dma((ITERS,)),
            ],
            compiler_params=pltpu.CompilerParams(
                collective_id=0, has_side_effects=True, vmem_limit_bytes=40 << 20
            ),
        )(*args)
        return pl.pallas_call(
            hand_over,
            out_shape=outs,
            in_specs=[vmem, vmem],
            out_specs=(hbm, hbm),
            scratch_shapes=[dma((2,))],
            compiler_params=pltpu.CompilerParams(vmem_limit_bytes=1 << 20),
        )(*results)

    pair = P(("cell", "grp"))
    wide = P(None, ("cell", "grp"))
    tall = P(("cell", "grp"), None)
    return jax.shard_map(
        step,
        mesh=mesh,
        in_specs=(wide, wide, wide, wide, pair, pair, pair, tall, tall, tall),
        out_specs=(wide, pair),
        check_vma=False,
    )
```

time: 35.4 us -> 30.1 us (0.85)
  Pallas kernels: 32.7 us -> 29.3 us
  local copies, waits for them, and re-layouts: 1.88 us -> 0 us
    pallas_call x1, Pallas kernels: 32.7 us -> 28.7 us  [step(): pl.pallas_call(functools.partial(body, (cells, grps, na, ng, nb, nq, nm))...]
    unnamed x4 -> x0, local copies, waits for them, and re-layouts: 1.88 us -> none
    pallas_call x0 -> x1, Pallas kernels: none -> 0.62 us  [step(): pl.pallas_call(hand_over, out_shape=outs, in_specs=[vmem, vmem], out_spec...]
where the time goes in v1:
time: 30.1 us; the launch traced here: 29.9 us
  Pallas kernels  29.3 us (97%)
  between operations  0.64 us (2%)
    pallas_call x1, Pallas kernels, step(): pl.pallas_call(functools.partial(body, (cells, grps, na, ng, nb, nq, nm))...  28.7 us
    pallas_call x1, Pallas kernels, step(): pl.pallas_call(hand_over, out_shape=outs, in_specs=[vmem, vmem], out_spec...  0.62 us

profile of v1, /device:TPU:0, one launch (start us, length us, event | category | flops | bytes accessed | tf_op | source)
XLA Modules:
  0.0 29.9 jit_solution(15586655862263430894)
XLA Ops:
  0.6 28.7 %shard_map.113 = (f32[3,512]{1,0:T(4,128)S(1)}, f32[384]{0:T(512)S(1)}) custom-call(s32[4,8]{1,0:T(4,128)} %refs_0_.1, s32[4,4]{1,0:T(4,128)} %refs_1_.1, s32[3,8]{1,0:T(4,128)} %refs_2_.1, f32[3,512]{1,0:T(4,128)} %refs_3_.1, f32[3,384]{1,0:T(4,128)} %refs_4_.1, f32[3,512]{1,0:T(4,128)} %refs_5_.1, f32[3,512]{1,0:T(4,128)} %refs_6_.1, f32[512]{0:T(512)} %refs_7_.1, ...), custom_call_target="tpu_custom_call" | custom-call | tf_op jit(solution)/shard_map/pallas_call | solution.py:480
  29.3 0.6 %shard_map.114 = (f32[3,512]{1,0:T(4,128)}, f32[384]{0:T(512)}) custom-call(f32[3,512]{1,0:T(4,128)S(1)} %get-tuple-element.4.dip, f32[384]{0:T(512)S(1)} %get-tuple-element.5.q), custom_call_target="tpu_custom_call" | custom-call | tf_op jit(solution)/shard_map/pallas_call | solution.py:512

commit v2 on v1

--- a/solution.py
+++ b/solution.py
@@ -29,11 +29,13 @@
     tab = refs[23 + 2 * ITERS : 23 + 3 * ITERS]
     rest = refs[23 + 3 * ITERS :]
     tgt_a, tgt_g, geo, sgeo, cgeo, pgeo, fgeo_a, fgeo_g, acc_a, acc_g = rest[:10]
-    load_sem, send_sem, recv_sem, far_send, far_recv = rest[10:]
+    load_sem, send_sem, recv_sem, far_send, far_recv, upward, downward = rest[10:]
     cell = lax.axis_index("cell")
     grp = lax.axis_index("grp")
     has_prev = cell > 0
     has_next = cell < cells - 1
+    has_prev2 = cell > 1
+    has_next2 = cell < cells - 2
     own = grps + grp
     cell_f = cell.astype(jnp.float32)
     centre = (cell_f + 0.5, 0.5, 0.5)
@@ -59,6 +61,28 @@
 
     def greet(c, g):
         pl.semaphore_signal(barrier, inc=1, device_id=(c, g), device_id_type=MESH)
+
+    def greet_near():
+        @pl.when(has_prev2)
+        def _():
+            greet(cell - 2, grp)
+
+        @pl.when(has_prev)
+        def _():
+            for d in order:
+                greet(cell - 1, lax.rem(grp + d, grps))
+
+        @pl.when(has_next)
+        def _():
+            for d in order:
+                greet(cell + 1, lax.rem(grp + d, grps))
+
+        for d in range(1, grps):
+            greet(cell, lax.rem(grp + d, grps))
+
+        @pl.when(has_next2)
+        def _():
+            greet(cell + 2, grp)
 
     def each_other_cell(act):
         def step(n, carry):
@@ -75,9 +99,7 @@
     ]
     for n in (3, 5, 4, 8, 0, 1, 2, 6, 7, 9):
         loads[n].start()
-    each_other_cell(greet)
-    for d in range(1, grps):
-        greet(cell, lax.rem(grp + d, grps))
+    greet_near()
 
     def clear(slot):
         for buf, rows, _ in [site_msg, point_msg] + mu_msg + charge_msg[1:]:
@@ -88,6 +110,18 @@
             tab[it][g * cells + cell] = jnp.zeros((1, BLOCK), jnp.float32)
     pl.when(jnp.logical_not(has_prev))(lambda: clear(0))
     pl.when(jnp.logical_not(has_next))(lambda: clear(2))
+
+    greeted = [(has_prev, grps), (has_next, grps), (has_prev2, 1), (has_next2, 1)]
+    pl.semaphore_wait(barrier, grps - 1 + sum(n * met.astype(jnp.int32) for met, n in greeted))
+    edge_up, edge_down = jnp.logical_not(has_prev2), jnp.logical_not(has_next2)
+
+    @pl.when(jnp.logical_and(edge_up, has_next2))
+    def _():
+        pl.semaphore_signal(upward, inc=1, device_id=(cell + 2, grp), device_id_type=MESH)
+
+    @pl.when(jnp.logical_and(edge_down, has_prev2))
+    def _():
+        pl.semaphore_signal(downward, inc=1, device_id=(cell - 2, grp), device_id_type=MESH)
 
     for n in (3, 5, 4, 8):
         loads[n].wait()
@@ -384,11 +418,27 @@
 
     atom_steps, grid_steps = na * HALVES, ng * HALVES
 
-    pl.semaphore_wait(barrier, cells * grps - 1)
     for_all(site_msg, start)
     for_all(mu_msg[0], start)
     for_all(point_msg, start)
     own_sums(0)
+
+    @pl.when(has_prev2)
+    def _():
+        pl.semaphore_wait(upward, 1)
+
+    @pl.when(jnp.logical_and(has_prev2, has_next2))
+    def _():
+        pl.semaphore_signal(upward, inc=1, device_id=(cell + 2, grp), device_id_type=MESH)
+
+    @pl.when(has_next2)
+    def _():
+        pl.semaphore_wait(downward, 1)
+
+    @pl.when(jnp.logical_and(has_prev2, has_next2))
+    def _():
+        pl.semaphore_signal(downward, inc=1, device_id=(cell - 2, grp), device_id_type=MESH)
+
     each_other_cell(lambda c, g: far_copy(0, c, g).start())
 
     for a in range(3):
@@ -504,6 +554,8 @@
                 dma((kinds, 3 * grps)),
                 dma((ITERS,)),
                 dma((ITERS,)),
+                pltpu.SemaphoreType.REGULAR,
+                pltpu.SemaphoreType.REGULAR,
             ],
             compiler_params=pltpu.CompilerParams(
                 collective_id=0, has_side_effects=True, vmem_limit_bytes=40 << 20

time: 30.1 us -> 28.7 us (0.953)
  Pallas kernels: 29.3 us -> 27.9 us
    pallas_call x1, Pallas kernels: 28.7 us -> 27.3 us  [step(): pl.pallas_call(functools.partial(body, (cells, grps, na, ng, nb, nq, nm))...]
where the time goes in v2:
time: 28.7 us; the launch traced here: 28.5 us
  Pallas kernels  27.9 us (97%)
  between operations  0.64 us (2%)
    pallas_call x1, Pallas kernels, step(): pl.pallas_call(functools.partial(body, (cells, grps, na, ng, nb, nq, nm))...  27.3 us
    pallas_call x1, Pallas kernels, step(): pl.pallas_call(hand_over, out_shape=outs, in_specs=[vmem, vmem], out_spec...  0.62 us

profile of v2, /device:TPU:0, one launch (start us, length us, event | category | flops | bytes accessed | tf_op | source)
XLA Modules:
  0.0 28.5 jit_solution(5468257481209838556)
XLA Ops:
  0.6 27.3 %shard_map.113 = (f32[3,512]{1,0:T(4,128)S(1)}, f32[384]{0:T(512)S(1)}) custom-call(s32[4,8]{1,0:T(4,128)} %refs_0_.1, s32[4,4]{1,0:T(4,128)} %refs_1_.1, s32[3,8]{1,0:T(4,128)} %refs_2_.1, f32[3,512]{1,0:T(4,128)} %refs_3_.1, f32[3,384]{1,0:T(4,128)} %refs_4_.1, f32[3,512]{1,0:T(4,128)} %refs_5_.1, f32[3,512]{1,0:T(4,128)} %refs_6_.1, f32[512]{0:T(512)} %refs_7_.1, ...), custom_call_target="tpu_custom_call" | custom-call | tf_op jit(solution)/shard_map/pallas_call | solution.py:530
  27.9 0.6 %shard_map.114 = (f32[3,512]{1,0:T(4,128)}, f32[384]{0:T(512)}) custom-call(f32[3,512]{1,0:T(4,128)S(1)} %get-tuple-element.4.dip, f32[384]{0:T(512)S(1)} %get-tuple-element.5.q), custom_call_target="tpu_custom_call" | custom-call | tf_op jit(solution)/shard_map/pallas_call | solution.py:564

commit v3 on v2

--- a/solution.py
+++ b/solution.py
@@ -84,14 +84,14 @@
         def _():
             greet(cell + 2, grp)
 
-    def each_other_cell(act):
-        def step(n, carry):
-            c = lax.rem(cell + n, cells)
-            for d in range(grps):
+    def each_far_cell(act):
+        def step(c, carry):
+            for d in order:
                 act(c, lax.rem(grp + d, grps))
             return carry
 
-        lax.fori_loop(1, cells, step, 0)
+        lax.fori_loop(0, cell - 1, step, 0)
+        lax.fori_loop(0, cells - 2 - cell, lambda n, carry: step(cells - 1 - n, carry), 0)
 
     loads = [
         pltpu.make_async_copy(src, dst, load_sem.at[n])
@@ -107,7 +107,8 @@
 
     for it in range(ITERS):
         for g in range(grps):
-            tab[it][g * cells + cell] = jnp.zeros((1, BLOCK), jnp.float32)
+            for c in (lax.max(cell - 1, 0), cell, lax.min(cell + 1, cells - 1)):
+                tab[it][g * cells + c] = jnp.zeros((1, BLOCK), jnp.float32)
     pl.when(jnp.logical_not(has_prev))(lambda: clear(0))
     pl.when(jnp.logical_not(has_next))(lambda: clear(2))
 
@@ -142,7 +143,7 @@
         dx, dy, dz = (t - s for t, s in zip(targets, source))
         inv = inverse_of(dx, dy, dz)
         cube = inv * inv * inv
-        weight = cube * lax.rsqrt(inv) * math.sqrt(3.0)
+        weight = inv * math.sqrt(3.0)
         ref[slot] = dx * weight
         ref[slot + 1] = dy * weight
         ref[slot + 2] = dz * weight
@@ -170,8 +171,8 @@
         return pltpu.make_async_remote_copy(
             src_ref=buf.at[pl.ds(own * rows, rows)],
             dst_ref=buf.at[pl.ds((slot * grps + grp) * rows, rows)],
-            send_sem=send_sem.at[kind, slot * grps + g],
-            recv_sem=recv_sem.at[kind, slot * grps + grp],
+            send_sem=send_sem.at[kind],
+            recv_sem=recv_sem.at[kind],
             device_id=(c, g),
             device_id_type=MESH,
         )
@@ -194,34 +195,35 @@
                 g = lax.rem(grp + d, grps)
                 act(piece_copy(msg, 1, cell, g))
 
-    def arrival(msg, p, c, g):
+    inner = jnp.logical_and(has_prev, has_next)
+
+    def traffic(msg, act):
         buf, rows, kind = msg
-        pltpu.make_async_remote_copy(
-            src_ref=buf.at[pl.ds(p * rows, rows)],
-            dst_ref=buf.at[pl.ds(p * rows, rows)],
-            send_sem=send_sem.at[kind, p],
-            recv_sem=recv_sem.at[kind, p],
-            device_id=(c, g),
-            device_id_type=MESH,
-        ).wait_recv()
+
+        def part(n):
+            some = buf.at[pl.ds(0, n * rows)]
+            act(
+                pltpu.make_async_remote_copy(
+                    src_ref=some,
+                    dst_ref=some,
+                    send_sem=send_sem.at[kind],
+                    recv_sem=recv_sem.at[kind],
+                    device_id=(cell, lax.rem(grp + 1, grps)),
+                    device_id_type=MESH,
+                )
+            )
+
+        pl.when(inner)(lambda: part(3 * grps - 1))
+        pl.when(jnp.logical_not(inner))(lambda: part(2 * grps - 1))
 
     def all_arrive(msg):
-        for d in range(1, grps):
-            g = lax.rem(grp + d, grps)
-            arrival(msg, grps + g, cell, g)
-
-        @pl.when(has_prev)
-        def _():
-            for g in range(grps):
-                arrival(msg, g, cell - 1, g)
-
-        @pl.when(has_next)
-        def _():
-            for g in range(grps):
-                arrival(msg, 2 * grps + g, cell + 1, g)
+        traffic(msg, arrive)
 
     def start(copy):
         copy.start()
+
+    def arrive(copy):
+        copy.wait_recv()
 
     def finish(copy):
         copy.wait_send()
@@ -239,8 +241,12 @@
             device_id_type=MESH,
         )
 
-    def far_all(it):
-        rows = tab[it].at[pl.ds(0, (cells - 1) * grps)]
+    def far_all(it, act):
+        pl.when(inner)(lambda: act(far_rows(it, cells - 3)))
+        pl.when(jnp.logical_not(inner))(lambda: act(far_rows(it, cells - 2)))
+
+    def far_rows(it, n):
+        rows = tab[it].at[pl.ds(0, n * grps)]
         return pltpu.make_async_remote_copy(
             src_ref=rows,
             dst_ref=rows,
@@ -324,7 +330,7 @@
             cube = sgeo[slot + 3]
             proj = u[0] * mu[0] + u[1] * mu[1] + u[2] * mu[2]
             for a in range(3):
-                acc_a[(i * UNROLL + t) * 3 + a] = u[a] * proj - cube * mu[a]
+                acc_a[(i * UNROLL + t) * 3 + a] = cube * (u[a] * proj - mu[a])
         return carry
 
     def near_atoms(it, i, carry):
@@ -338,7 +344,7 @@
                 cube = geo[slot + 3]
                 proj = u[0] * mu[0] + u[1] * mu[1] + u[2] * mu[2]
                 for a in range(3):
-                    acc[t][a] = acc[t][a] + (u[a] * proj - cube * mu[a])
+                    acc[t][a] = acc[t][a] + cube * (u[a] * proj - mu[a])
         for t in range(UNROLL):
             for a in range(3):
                 acc_a[(i * UNROLL + t) * 3 + a] = acc[t][a]
@@ -416,6 +422,17 @@
             else:
                 out_q[b * BLOCK : (b + 1) * BLOCK] = new.reshape(BLOCK)
 
+    def repeat(n, chunk, fn):
+        def step(j, carry):
+            for m in range(chunk):
+                fn(j * chunk + m, carry)
+            return carry
+
+        if chunk == n:
+            step(0, 0)
+        else:
+            lax.fori_loop(0, n // chunk, step, 0)
+
     atom_steps, grid_steps = na * HALVES, ng * HALVES
 
     for_all(site_msg, start)
@@ -439,7 +456,7 @@
     def _():
         pl.semaphore_signal(downward, inc=1, device_id=(cell - 2, grp), device_id_type=MESH)
 
-    each_other_cell(lambda c, g: far_copy(0, c, g).start())
+    each_far_cell(lambda c, g: far_copy(0, c, g).start())
 
     for a in range(3):
         for b in range(na):
@@ -450,7 +467,7 @@
         source = [wide(vec_row(sites, a, b)) for a in range(3)]
         for t in range(GROUPS):
             store_dipole_pair(sgeo, (b * GROUPS + t) * 4, targets_of(tgt_a, b, t), source, diag == t * SUB)
-    lax.fori_loop(0, atom_steps, functools.partial(self_atoms, 0), 0)
+    repeat(atom_steps, 4, functools.partial(self_atoms, 0))
     for b in range(na):
         store_far(fgeo_a, b, lambda a: vec_row(sites, a, b))
     for b in range(ng):
@@ -459,39 +476,42 @@
         loads[n].wait()
 
     all_arrive(site_msg)
-    lax.fori_loop(0, atom_steps, near_geometry, 0)
+    repeat(atom_steps, 4, near_geometry)
 
     for it in range(ITERS):
         last = it + 1 == ITERS
         all_arrive(mu_msg[it])
-        lax.fori_loop(0, atom_steps, functools.partial(near_atoms, it), 0)
-        if last:
-            lax.fori_loop(0, grid_steps, functools.partial(near_grid, it), 0)
+        repeat(atom_steps, 4, functools.partial(near_atoms, it))
+        if it:
+            repeat(grid_steps, 3, functools.partial(near_grid, it))
         if it == 0:
             all_arrive(point_msg)
-            lax.fori_loop(0, atom_steps, charge_geometry, 0)
+            repeat(atom_steps, 4, charge_geometry)
         else:
             all_arrive(charge_msg[it])
-        far_all(it).wait_recv()
+        atom_near = atom_fields(it)
+        grid_near = grid_fields() if it else None
+        far_all(it, arrive)
         sums = far_sums(it)
-        finish_atoms(it, atom_fields(it), sums)
+        finish_atoms(it, atom_near, sums)
         if last:
-            finish_grid(it, grid_fields(), sums)
+            finish_grid(it, grid_near, sums)
             break
         for_all(mu_msg[it + 1], start)
         if it == 0:
-            lax.fori_loop(0, grid_steps, grid_geometry, 0)
-        lax.fori_loop(0, grid_steps, functools.partial(near_grid, it), 0)
-        finish_grid(it, grid_fields(), sums)
+            repeat(grid_steps, 3, grid_geometry)
+            repeat(grid_steps, 3, functools.partial(near_grid, it))
+            grid_near = grid_fields()
+        finish_grid(it, grid_near, sums)
+        own_sums(it + 1)
+        each_far_cell(lambda c, g: far_copy(it + 1, c, g).start())
         for_all(charge_msg[it + 1], start)
-        own_sums(it + 1)
-        each_other_cell(lambda c, g: far_copy(it + 1, c, g).start())
-        lax.fori_loop(0, atom_steps, functools.partial(self_atoms, it + 1), 0)
+        repeat(atom_steps, 4, functools.partial(self_atoms, it + 1))
 
     for msg in [site_msg, point_msg] + mu_msg + charge_msg[1:]:
-        for_all(msg, finish)
+        traffic(msg, finish)
     for it in range(ITERS):
-        far_all(it).wait_send()
+        far_all(it, finish)
 
 
 def hand_over(dip, q, out_dip, out_q, sem):
@@ -550,8 +570,8 @@
                 tiles(na * GROUPS * 3),
                 tiles(ng * GROUPS),
                 dma((10,)),
-                dma((kinds, 3 * grps)),
-                dma((kinds, 3 * grps)),
+                dma((kinds,)),
+                dma((kinds,)),
                 dma((ITERS,)),
                 dma((ITERS,)),
                 pltpu.SemaphoreType.REGULAR,

time: 28.7 us -> 26.4 us (0.920)
  Pallas kernels: 27.9 us -> 25.6 us
    pallas_call x1, Pallas kernels: 27.3 us -> 25 us  [step(): pl.pallas_call(functools.partial(body, (cells, grps, na, ng, nb, nq, nm))...]
where the time goes in v3:
time: 26.4 us; the launch traced here: 26.3 us
  Pallas kernels  25.6 us (97%)
  between operations  0.64 us (2%)
    pallas_call x1, Pallas kernels, step(): pl.pallas_call(functools.partial(body, (cells, grps, na, ng, nb, nq, nm))...  25 us
    pallas_call x1, Pallas kernels, step(): pl.pallas_call(hand_over, out_shape=outs, in_specs=[vmem, vmem], out_spec...  0.62 us

profile of v3, /device:TPU:0, one launch (start us, length us, event | category | flops | bytes accessed | tf_op | source)
XLA Modules:
  0.0 26.3 jit_solution(15580053577084615498)
XLA Ops:
  0.6 25.0 %shard_map.113 = (f32[3,512]{1,0:T(4,128)S(1)}, f32[384]{0:T(512)S(1)}) custom-call(s32[4,8]{1,0:T(4,128)} %refs_0_.1, s32[4,4]{1,0:T(4,128)} %refs_1_.1, s32[3,8]{1,0:T(4,128)} %refs_2_.1, f32[3,512]{1,0:T(4,128)} %refs_3_.1, f32[3,384]{1,0:T(4,128)} %refs_4_.1, f32[3,512]{1,0:T(4,128)} %refs_5_.1, f32[3,512]{1,0:T(4,128)} %refs_6_.1, f32[512]{0:T(512)} %refs_7_.1, ...), custom_call_target="tpu_custom_call" | custom-call | tf_op jit(solution)/shard_map/pallas_call | solution.py:550
  25.7 0.6 %shard_map.114 = (f32[3,512]{1,0:T(4,128)}, f32[384]{0:T(512)}) custom-call(f32[3,512]{1,0:T(4,128)S(1)} %get-tuple-element.4.dip, f32[384]{0:T(512)S(1)} %get-tuple-element.5.q), custom_call_target="tpu_custom_call" | custom-call | tf_op jit(solution)/shard_map/pallas_call | solution.py:584

commit v4 on v3

--- a/solution.py
+++ b/solution.py
@@ -277,9 +277,14 @@
         tab[it][grp * cells + cell] = column_sum(jnp.where(diag == 0, sums, 0.0))
 
     def far_sums(it):
-        total = tab[it][0:cells, 0, :]
-        for g in range(1, grps):
-            total = total + tab[it][g * cells : (g + 1) * cells, 0, :]
+        parts = []
+        for first in range(0, cells, SUB):
+            part = jnp.zeros((SUB, BLOCK), jnp.float32)
+            for c in range(first, min(first + SUB, cells)):
+                row = functools.reduce(jnp.add, [wide(tab[it][g * cells + c]) for g in range(grps)])
+                part = jnp.where(subs == c - first, row, part)
+            parts.append(part)
+        total = jnp.concatenate(parts, axis=0)[:cells]
         return [jnp.broadcast_to(total[:, n : n + 1], (cells, BLOCK)) for n in range(7)]
 
     def site_rows(w):

time: 26.4 us -> 26.1 us (0.989)
  Pallas kernels: 25.6 us -> 25.3 us
    pallas_call x1, Pallas kernels: 25 us -> 24.7 us  [step(): pl.pallas_call(functools.partial(body, (cells, grps, na, ng, nb, nq, nm))...]
where the time goes in v4:
time: 26.1 us; the launch traced here: 25.9 us
  Pallas kernels  25.3 us (97%)
  between operations  0.64 us (2%)
    pallas_call x1, Pallas kernels, step(): pl.pallas_call(functools.partial(body, (cells, grps, na, ng, nb, nq, nm))...  24.7 us
    pallas_call x1, Pallas kernels, step(): pl.pallas_call(hand_over, out_shape=outs, in_specs=[vmem, vmem], out_spec...  0.62 us

profile of v4, /device:TPU:0, one launch (start us, length us, event | category | flops | bytes accessed | tf_op | source)
XLA Modules:
  0.0 25.9 jit_solution(9039131371744169561)
XLA Ops:
  0.6 24.7 %shard_map.113 = (f32[3,512]{1,0:T(4,128)S(1)}, f32[384]{0:T(512)S(1)}) custom-call(s32[4,8]{1,0:T(4,128)} %refs_0_.1, s32[4,4]{1,0:T(4,128)} %refs_1_.1, s32[3,8]{1,0:T(4,128)} %refs_2_.1, f32[3,512]{1,0:T(4,128)} %refs_3_.1, f32[3,384]{1,0:T(4,128)} %refs_4_.1, f32[3,512]{1,0:T(4,128)} %refs_5_.1, f32[3,512]{1,0:T(4,128)} %refs_6_.1, f32[512]{0:T(512)} %refs_7_.1, ...), custom_call_target="tpu_custom_call" | custom-call | tf_op jit(solution)/shard_map/pallas_call | solution.py:555
  25.3 0.6 %shard_map.114 = (f32[3,512]{1,0:T(4,128)}, f32[384]{0:T(512)}) custom-call(f32[3,512]{1,0:T(4,128)S(1)} %get-tuple-element.4.dip, f32[384]{0:T(512)S(1)} %get-tuple-element.5.q), custom_call_target="tpu_custom_call" | custom-call | tf_op jit(solution)/shard_map/pallas_call | solution.py:589

commit v5 on v4

--- a/solution.py
+++ b/solution.py
@@ -28,8 +28,8 @@
     chg = (None,) + refs[24 + ITERS : 23 + 2 * ITERS]
     tab = refs[23 + 2 * ITERS : 23 + 3 * ITERS]
     rest = refs[23 + 3 * ITERS :]
-    tgt_a, tgt_g, geo, sgeo, cgeo, pgeo, fgeo_a, fgeo_g, acc_a, acc_g = rest[:10]
-    load_sem, send_sem, recv_sem, far_send, far_recv, upward, downward = rest[10:]
+    tgt_a, tgt_g, geo, sgeo, cgeo, pgeo, fgeo_a, fgeo_g, acc_a, acc_g, kept = rest[:11]
+    load_sem, send_sem, recv_sem, far_send, far_recv, upward, downward = rest[11:]
     cell = lax.axis_index("cell")
     grp = lax.axis_index("grp")
     has_prev = cell > 0
@@ -410,7 +410,7 @@
             radial = radial + sums[3] * cube
             for a in range(3):
                 far = column_sum(radial * delta[a] - moments[a] * cube)
-                new = flat_row(pol, b) * (vec_row(fixed, a, b) + (near[b][a] + far))
+                new = kept[b * 3 + a] + flat_row(pol, b) * far
                 if it + 1 < ITERS:
                     mus[it + 1][own * 3 * na + b * 3 + a] = new
                 else:
@@ -421,7 +421,10 @@
             delta = [fgeo_g[b * 5 + a] for a in range(3)]
             proj = sums[0] * delta[0] + sums[1] * delta[1] + sums[2] * delta[2]
             far = column_sum(proj * fgeo_g[b * 5 + 3])
-            new = flat_row(base, b) - flat_row(resp, b) * (near[b] + far)
+            if it:
+                new = kept[na * 3 + b] - flat_row(resp, b) * far
+            else:
+                new = flat_row(base, b) - flat_row(resp, b) * (near[b] + far)
             if it + 1 < ITERS:
                 chg[it + 1][own * ng + b] = new
             else:
@@ -496,6 +499,12 @@
             all_arrive(charge_msg[it])
         atom_near = atom_fields(it)
         grid_near = grid_fields() if it else None
+        for b in range(na):
+            for a in range(3):
+                kept[b * 3 + a] = flat_row(pol, b) * (vec_row(fixed, a, b) + atom_near[b][a])
+        if it:
+            for b in range(ng):
+                kept[na * 3 + b] = flat_row(base, b) - flat_row(resp, b) * grid_near[b]
         far_all(it, arrive)
         sums = far_sums(it)
         finish_atoms(it, atom_near, sums)
@@ -574,6 +583,7 @@
                 tiles(ng * 5, cells),
                 tiles(na * GROUPS * 3),
                 tiles(ng * GROUPS),
+                pltpu.VMEM((na * 3 + ng, 1, BLOCK), f32),
                 dma((10,)),
                 dma((kinds,)),
                 dma((kinds,)),

time: 26.1 us -> 26.1 us (level)
  no operation moved by 1% of the time
where the time goes in v5:
time: 26.1 us; the launch traced here: 26 us
  Pallas kernels  25.3 us (97%)
  between operations  0.64 us (2%)
    pallas_call x1, Pallas kernels, step(): pl.pallas_call(functools.partial(body, (cells, grps, na, ng, nb, nq, nm))...  24.7 us
    pallas_call x1, Pallas kernels, step(): pl.pallas_call(hand_over, out_shape=outs, in_specs=[vmem, vmem], out_spec...  0.62 us

profile of v5, /device:TPU:0, one launch (start us, length us, event | category | flops | bytes accessed | tf_op | source)
XLA Modules:
  0.0 26.0 jit_solution(15531122793356992039)
XLA Ops:
  0.6 24.7 %shard_map.113 = (f32[3,512]{1,0:T(4,128)S(1)}, f32[384]{0:T(512)S(1)}) custom-call(s32[4,8]{1,0:T(4,128)} %refs_0_.1, s32[4,4]{1,0:T(4,128)} %refs_1_.1, s32[3,8]{1,0:T(4,128)} %refs_2_.1, f32[3,512]{1,0:T(4,128)} %refs_3_.1, f32[3,384]{1,0:T(4,128)} %refs_4_.1, f32[3,512]{1,0:T(4,128)} %refs_5_.1, f32[3,512]{1,0:T(4,128)} %refs_6_.1, f32[512]{0:T(512)} %refs_7_.1, ...), custom_call_target="tpu_custom_call" | custom-call | tf_op jit(solution)/shard_map/pallas_call | solution.py:564
  25.4 0.6 %shard_map.114 = (f32[3,512]{1,0:T(4,128)}, f32[384]{0:T(512)}) custom-call(f32[3,512]{1,0:T(4,128)S(1)} %get-tuple-element.4.dip, f32[384]{0:T(512)S(1)} %get-tuple-element.5.q), custom_call_target="tpu_custom_call" | custom-call | tf_op jit(solution)/shard_map/pallas_call | solution.py:599
